TPU v7x, 32 devices: a whole 2x2x4 slice. The times are simulated.
32 devices in a mesh: row: 2 (over x), col: 4 (over y, core), depth: 4 (over z).
Axes of the slice: x: 2, y: 2, z: 4, core: 2. Of those that a mesh axis runs over, the one named last changes fastest.
Arguments:
- left_values: bfloat16 [96, 32, 4, 529], P('row', ('col', 'depth')), may hold values from -1.25 to 1.25
- left_columns: int32 [96, 32, 4], P('row', ('col', 'depth')), may hold values from 0 to 39, as said below
- right_values: bfloat16 [32, 40, 4, 3, 529], P(('col', 'depth'), 'row'), may hold values from -1.75 to 1.75
- right_columns: int32 [32, 40, 4, 3], P(('col', 'depth'), 'row'), may hold values from 0 to 31, as said below
Outputs:
- product_matrix: bfloat16 [2208, 2944], P('row', ('col', 'depth'))
Inputs may be any that keep to these rules, and one draw needn't show every extreme that they name: `left_columns`: within one block row and panel the 4 entries are distinct. `right_columns`: within one block row and column tile the 3 entries are distinct.
All inputs are finite; a program needn't handle non-finite values.
Results may differ from a plain program's by a relative error of at most 0.001.
Values may be sent and summed in bfloat16 or wider, within the bound.
A program may use at most 192 MiB of HBM per device.

v0:
```python
import math
import jax
import jax.numpy as jnp
from jax import lax
from jax.sharding import PartitionSpec as P

PANEL = 40
CTW = 32


def dense_left(values, columns, panel_width):
    rows_here, panels, slots, square = values.shape
    block_edge = math.isqrt(square)
    onehot = (
        columns.astype(jnp.float32)[..., None] == jnp.arange(panel_width, dtype=jnp.float32)
    ).astype(jnp.bfloat16)
    blocks = values.reshape(rows_here, panels, slots, block_edge, block_edge)
    filled = jnp.einsum(
        "mqsp,mqsab->qmapb", onehot, blocks, preferred_element_type=jnp.float32
    ).astype(jnp.bfloat16)
    return filled.reshape(panels, rows_here * block_edge, panel_width * block_edge)


def dense_right(values, columns, tile_width):
    panels, rows_here, tiles, slots, square = values.shape
    block_edge = math.isqrt(square)
    onehot = (
        columns.astype(jnp.float32)[..., None] == jnp.arange(tile_width, dtype=jnp.float32)
    ).astype(jnp.bfloat16)
    blocks = values.reshape(panels, rows_here, tiles, slots, block_edge, block_edge)
    filled = jnp.einsum(
        "qrtuc,qrtuab->qratcb", onehot, blocks, preferred_element_type=jnp.float32
    ).astype(jnp.bfloat16)
    return filled.reshape(panels, rows_here * block_edge, tiles * tile_width * block_edge)


def contract(left_values, left_codes, right_values, right_codes):
    left_filled = dense_left(left_values, left_codes, PANEL)
    right_filled = dense_right(
        lax.all_gather(right_values, "row", axis=1, tiled=True),
        lax.all_gather(right_codes, "row", axis=1, tiled=True),
        CTW,
    )
    return jnp.einsum("qmk,qkn->mn", left_filled, right_filled, preferred_element_type=jnp.float32)


def body(left_values, left_columns, right_values, right_columns):
    right_codes = right_columns.astype(jnp.bfloat16)
    partial_sums = contract(left_values, left_columns, right_values, right_codes)
    result = lax.psum_scatter(partial_sums, ("col", "depth"), scatter_dimension=1, tiled=True)
    return result.astype(jnp.bfloat16)


def solution(mesh):
    placed = (
        P("row", ("col", "depth"), None, None),
        P("row", ("col", "depth"), None),
        P(("col", "depth"), "row", None, None, None),
        P(("col", "depth"), "row", None, None),
    )
    return jax.shard_map(
        body, mesh=mesh, in_specs=placed, out_specs=P("row", ("col", "depth")), check_vma=False
    )
```

profile of v0, /device:TPU:0, one launch (start us, length us, event | category | flops | bytes accessed | tf_op | source)
XLA Modules:
  0.0 491.5 jit_solution(12231086556347016809)
XLA Ops:
  6.5 0.0 reduce-scatter.4.cloned.1.call-start
  6.5 21.0 %all_gather.7 = bf16[2,40,4,3,529]{4,2,3,1,0:T(4,128)(2,1)} all-gather(bf16[2,20,4,3,529]{4,2,3,1,0:T(4,128)(2,1)} %param.6), channel_id=1, replica_groups=mesh['row'=2,'col'=4,'depth'=4] {'row'}, dimensions={1}, use_global_device_ids=true | all-gather | bytes 1523520 | tf_op jit(solution)/shard_map/all_gather | solution.py:40
  27.5 0.0 copy-start.1
  27.5 4.9 %copy.32 = bf16[2,40,4,3,529]{1,2,4,3,0:T(4,128)(2,1)S(1)} copy(bf16[2,40,4,3,529]{4,2,3,1,0:T(4,128)(2,1)} %all_gather.7) | data formatting | bytes 2031360 | tf_op jit(solution)/shard_map/all_gather | solution.py:40
  32.4 11.9 %copy.33 = bf16[2,40,4,3,23,23]{5,3,4,2,1,0:T(4,128)(2,1)} copy(bf16[2,40,4,3,23,23]{1,2,5,4,3,0:T(4,128)(2,1)S(1)} %bitcast.33) | data formatting | bytes 2031360 | tf_op jit(solution)/shard_map/reshape | solution.py:30
  44.3 0.0 copy-done.1
  44.3 0.1 copy.29
  44.4 4.5 all_gather.6
  49.0 0.1 copy.30
  49.1 0.2 copy.31
  49.3 31.1 %convert_bitcast_fusion = bf16[2,40,23,4,32,23]{4,5,2,3,1,0:T(8,128)(2,1)} fusion(bf16[2,40,4,3,23,23]{5,3,4,2,1,0:T(4,128)(2,1)} %copy.33, f32[2,40,4,3]{3,2,1,0:T(4,128)S(1)} %copy.31), kind=kOutput, calls=%fused_computation | convolution fusion | flops 37949440 | bytes 11853440 | tf_op jit(solution)/shard_map/qrtuc,qrtuab->qratcb/dot_general | solution.py:31
  80.4 80.8 %copy.34 = bf16[2,40,23,4,32,23]{5,4,3,2,1,0:T(8,128)(2,1)} copy(bf16[2,40,23,4,32,23]{4,5,2,3,1,0:T(8,128)(2,1)} %convert_bitcast_fusion) | data formatting | bytes 21667840 | tf_op jit(solution)/shard_map/convert_element_type | solution.py:33
  161.2 0.0 copy-start
  161.2 0.0 copy-start.2
  161.2 70.7 %reshape.17 = bf16[2,920,2944]{2,1,0:T(8,128)(2,1)} reshape(bf16[2,40,23,4,32,23]{5,4,3,2,1,0:T(8,128)(2,1)} %copy.34) | data formatting | bytes 21667840 | tf_op jit(solution)/shard_map/reshape | solution.py:34
  231.9 0.0 copy-done
  231.9 1.7 copy.26
  233.6 3.6 copy.27
  237.2 0.0 copy-done.2
  237.2 0.1 copy.25
  237.3 10.2 %fusion = bf16[2,48,23,40,23]{3,4,2,1,0:T(8,128)(2,1)} fusion(bf16[48,2,4,23,23]{4,2,3,0,1:T(4,128)(2,1)S(1)} %copy.27, f32[48,2,4]{2,0,1:T(8,128)S(1)} %copy.25), kind=kOutput, calls=%fused_computation.3 | convolution fusion | flops 18297600 | bytes 4470528 | tf_op jit(solution)/shard_map/mqsp,mqsab->qmapb/dot_general | solution.py:18
  247.5 45.4 %copy.28 = bf16[2,48,23,40,23]{2,1,4,3,0:T(8,128)(2,1)} copy(bf16[2,48,23,40,23]{3,4,2,1,0:T(8,128)(2,1)} %fusion) | data formatting | bytes 8125440 | tf_op jit(solution)/shard_map/convert_element_type | solution.py:20
  292.9 27.5 %reshape.15 = bf16[2,1104,920]{1,2,0:T(8,128)(2,1)} reshape(bf16[2,48,23,40,23]{2,1,4,3,0:T(8,128)(2,1)} %copy.28) | data formatting | bytes 8125440 | tf_op jit(solution)/shard_map/reshape | solution.py:21
  320.3 21.8 %convolution_bitcast_fusion = f32[1104,2944]{0,1:T(8,128)} fusion(bf16[2,1104,920]{1,2,0:T(8,128)(2,1)} %reshape.15, bf16[2,920,2944]{2,1,0:T(8,128)(2,1)} %reshape.17), kind=kOutput, calls=%fused_computation.2 | convolution fusion | flops 11960647680 | bytes 27897344 | tf_op jit(solution)/shard_map/qmk,qkn->mn/dot_general | solution.py:44
  342.1 0.0 reduce-scatter.4.cloned.1.call-update
  342.1 140.6 %reduce-scatter.4.cloned.1.call-done = f32[1104,184]{0,1:T(8,128)} async-done(((f32[1104,2944]{0,1:T(8,128)}), f32[1104,184]{0,1:T(8,128)}) %reduce-scatter.4.cloned.1.call-update) | async-done | bytes 812560
  482.7 2.0 convert_element_type.33
  (2 shorter events, 0.0 us)
Async XLA Ops:
  6.5 476.1 %reduce-scatter.4.cloned.1.call-start = ((), (), s32[]{:S(2)}) async-start(), calls=%async_computation.1 | async-start | bytes 14413824
  27.5 16.8 %copy-start.1 = (s32[2,20,4,3]{1,2,3,0:T(4,128)S(1)}, s32[2,20,4,3]{1,2,3,0:T(4,128)}, u32[]{:S(2)}) copy-start(s32[2,20,4,3]{1,2,3,0:T(4,128)} %param.7) | copy-start | bytes 5764
  161.2 70.7 %copy-start = (bf16[48,2,4,529]{3,2,1,0:T(4,128)(2,1)S(1)}, bf16[48,2,4,529]{3,2,1,0:T(4,128)(2,1)}, u32[]{:S(2)}) copy-start(bf16[48,2,4,529]{3,2,1,0:T(4,128)(2,1)} %param.4) | copy-start | bytes 1218820
  161.2 75.9 %copy-start.2 = (s32[48,2,4]{0,2,1:T(4,128)S(1)}, s32[48,2,4]{0,2,1:T(4,128)}, u32[]{:S(2)}) copy-start(s32[48,2,4]{0,2,1:T(4,128)} %param.5) | copy-start | bytes 4612
Sparse Core Ops, SparseCore 0:
  342.2 140.3 reduce-scatter.3
where the time goes:
time: 497 us; the launch traced here: 491 us
  local copies, waits for them, and re-layouts  247 us (50%)
  waiting for transfers between devices  141 us (28%)
  matrix products  63.1 us (13%)
  blocking collectives  25.5 us (5%)
  between operations  13.4 us (3%)
    unnamed x2, waiting for transfers between devices  141 us
    convert_element_type x1, local copies, waits for them, and re-layouts, dense_right(): filled = jnp.einsum('qrtuc,qrtuab->qratcb', onehot, blocks, preferred_ele...  80.8 us
    reshape x1, local copies, waits for them, and re-layouts, dense_right(): filled.reshape(panels, rows_here * block_edge, tiles * tile_width * block...  70.7 us
    convert_element_type x1, local copies, waits for them, and re-layouts, dense_left(): filled = jnp.einsum('mqsp,mqsab->qmapb', onehot, blocks, preferred_elemen...  45.4 us
    dot_general x1, matrix products, dense_right(): jnp.einsum('qrtuc,qrtuab->qratcb', onehot, blocks, preferred_element_type...  31.1 us
    reshape x1, local copies, waits for them, and re-layouts, dense_left(): filled.reshape(panels, rows_here * block_edge, panel_width * block_edge)  27.5 us
    dot_general x1, matrix products, contract(): jnp.einsum('qmk,qkn->mn', left_filled, right_filled, preferred_element_ty...  21.8 us
    all_gather x1, blocking collectives, contract(): lax.all_gather(right_values, 'row', axis=1, tiled=True)  21 us
  transfers between devices with their start and end apart: 1, of which 1 were waited for; matrix products, arithmetic and copies ran while one was open for 0% of the time, Pallas kernels for 0%

commit v1 on v0

--- a/solution.py
+++ b/solution.py
@@ -6,6 +6,12 @@
 
 PANEL = 40
 CTW = 32
+
+
+def gathered_along(x, axis, dim):
+    parts = lax.all_gather(x, axis, axis=0, tiled=False)
+    full = jnp.concatenate(parts, axis=dim)
+    return full
 
 
 def dense_left(values, columns, panel_width):
@@ -37,7 +43,7 @@
 def contract(left_values, left_codes, right_values, right_codes):
     left_filled = dense_left(left_values, left_codes, PANEL)
     right_filled = dense_right(
-        lax.all_gather(right_values, "row", axis=1, tiled=True),
+        gathered_along(right_values, "row", 1),
         lax.all_gather(right_codes, "row", axis=1, tiled=True),
         CTW,
     )

time: 497 us -> 486 us (0.978)
  local copies, waits for them, and re-layouts: 247 us -> 237 us
    reshape x1 -> x0, local copies, waits for them, and re-layouts: 11.9 us -> none  [dense_right(): values.reshape(panels, rows_here, tiles, slots, block_edge, block_edge)]
    another operation x0 -> x1, local copies, waits for them, and re-layouts: none -> 6.59 us  [dense_right(): values.reshape(panels, rows_here, tiles, slots, block_edge, block_edge)]
where the time goes in v1:
time: 486 us; the launch traced here: 480 us
  local copies, waits for them, and re-layouts  237 us (49%)
  waiting for transfers between devices  142 us (29%)
  matrix products  62.7 us (13%)
  blocking collectives  22.4 us (5%)
  between operations  13.4 us (3%)
    unnamed x2, waiting for transfers between devices  142 us
    convert_element_type x1, local copies, waits for them, and re-layouts, dense_right(): filled = jnp.einsum('qrtuc,qrtuab->qratcb', onehot, blocks, preferred_ele...  80.8 us
    reshape x1, local copies, waits for them, and re-layouts, dense_right(): filled.reshape(panels, rows_here * block_edge, tiles * tile_width * block...  70.7 us
    convert_element_type x1, local copies, waits for them, and re-layouts, dense_left(): filled = jnp.einsum('mqsp,mqsab->qmapb', onehot, blocks, preferred_elemen...  45.4 us
    dot_general x1, matrix products, dense_right(): jnp.einsum('qrtuc,qrtuab->qratcb', onehot, blocks, preferred_element_type...  30.8 us
    reshape x1, local copies, waits for them, and re-layouts, dense_left(): filled.reshape(panels, rows_here * block_edge, panel_width * block_edge)  27.5 us
    dot_general x1, matrix products, contract(): jnp.einsum('qmk,qkn->mn', left_filled, right_filled, preferred_element_ty...  21.7 us
    all_gather x1, blocking collectives, gathered_along(): parts = lax.all_gather(x, axis, axis=0, tiled=False)  17.9 us
  transfers between devices with their start and end apart: 1, of which 1 were waited for; matrix products, arithmetic and copies ran while one was open for 0% of the time, Pallas kernels for 0%

profile of v1, /device:TPU:0, one launch (start us, length us, event | category | flops | bytes accessed | tf_op | source)
XLA Modules:
  0.0 480.0 jit_solution(10411567976000572632)
XLA Ops:
  6.5 0.0 copy-start.1
  6.5 0.0 reduce-scatter.4.cloned.1.call-start
  6.5 17.9 %all-gather = bf16[4,20,4,3,529]{4,2,3,1,0:T(4,128)(2,1)S(1)} all-gather(bf16[2,20,4,3,529]{4,2,3,1,0:T(4,128)(2,1)} %param.6), channel_id=2, replica_groups=mesh['row'=2,'col'=4,'depth'=4] {'row'}, dimensions={0}, use_global_device_ids=true | all-gather | bytes 1523520 | tf_op jit(solution)/shard_map/all_gather | solution.py:12
  24.4 0.4 copy.41
  24.8 6.6 %reshape_reshape.3 = bf16[2,40,4,3,23,23]{5,4,2,3,1,0:T(8,128)(2,1)} reshape(bf16[2,2,20,4,3,529]{5,3,4,2,1,0:T(4,128)(2,1)S(1)} %bitcast.36) | data formatting | bytes 2031360 | tf_op jit(solution)/shard_map/reshape;reshape | solution.py:36
  31.4 0.0 copy-done.1
  31.4 0.1 copy.29
  31.6 4.5 all_gather.9
  36.1 0.1 copy.30
  36.3 0.2 copy.31
  36.4 30.8 %convert_bitcast_fusion = bf16[2,40,23,4,32,23]{4,5,2,3,1,0:T(8,128)(2,1)} fusion(bf16[2,40,4,3,23,23]{5,4,2,3,1,0:T(8,128)(2,1)} %reshape_reshape.3, f32[2,40,4,3]{3,2,1,0:T(4,128)S(1)} %copy.31), kind=kOutput, calls=%fused_computation | convolution fusion | flops 37949440 | bytes 11853440 | tf_op jit(solution)/shard_map/qrtuc,qrtuab->qratcb/dot_general | solution.py:37
  67.2 80.8 %copy.34 = bf16[2,40,23,4,32,23]{5,4,3,2,1,0:T(8,128)(2,1)} copy(bf16[2,40,23,4,32,23]{4,5,2,3,1,0:T(8,128)(2,1)} %convert_bitcast_fusion) | data formatting | bytes 21667840 | tf_op jit(solution)/shard_map/convert_element_type | solution.py:39
  148.0 0.0 copy-start
  148.0 0.0 copy-start.2
  148.0 70.7 %reshape.17 = bf16[2,920,2944]{2,1,0:T(8,128)(2,1)} reshape(bf16[2,40,23,4,32,23]{5,4,3,2,1,0:T(8,128)(2,1)} %copy.34) | data formatting | bytes 21667840 | tf_op jit(solution)/shard_map/reshape | solution.py:40
  218.7 0.0 copy-done
  218.7 1.7 copy.26
  220.4 3.6 copy.27
  223.9 0.0 copy-done.2
  223.9 0.1 copy.25
  224.0 10.2 %fusion = bf16[2,48,23,40,23]{3,4,2,1,0:T(8,128)(2,1)} fusion(bf16[48,2,4,23,23]{4,2,3,0,1:T(4,128)(2,1)S(1)} %copy.27, f32[48,2,4]{2,0,1:T(8,128)S(1)} %copy.25), kind=kOutput, calls=%fused_computation.3 | convolution fusion | flops 18297600 | bytes 4470528 | tf_op jit(solution)/shard_map/mqsp,mqsab->qmapb/dot_general | solution.py:24
  234.2 45.4 %copy.28 = bf16[2,48,23,40,23]{2,1,4,3,0:T(8,128)(2,1)} copy(bf16[2,48,23,40,23]{3,4,2,1,0:T(8,128)(2,1)} %fusion) | data formatting | bytes 8125440 | tf_op jit(solution)/shard_map/convert_element_type | solution.py:26
  279.6 27.5 %reshape.15 = bf16[2,1104,920]{1,2,0:T(8,128)(2,1)} reshape(bf16[2,48,23,40,23]{2,1,4,3,0:T(8,128)(2,1)} %copy.28) | data formatting | bytes 8125440 | tf_op jit(solution)/shard_map/reshape | solution.py:27
  307.1 21.7 %convolution_bitcast_fusion = f32[1104,2944]{0,1:T(8,128)} fusion(bf16[2,1104,920]{1,2,0:T(8,128)(2,1)} %reshape.15, bf16[2,920,2944]{2,1,0:T(8,128)(2,1)} %reshape.17), kind=kOutput, calls=%fused_computation.2 | convolution fusion | flops 11960647680 | bytes 27897344 | tf_op jit(solution)/shard_map/qmk,qkn->mn/dot_general | solution.py:50
  328.8 0.0 reduce-scatter.4.cloned.1.call-update
  328.9 142.4 %reduce-scatter.4.cloned.1.call-done = f32[1104,184]{0,1:T(8,128)} async-done(((f32[1104,2944]{0,1:T(8,128)}), f32[1104,184]{0,1:T(8,128)}) %reduce-scatter.4.cloned.1.call-update) | async-done | bytes 812560
  471.2 2.0 convert_element_type.33
  (2 shorter events, 0.0 us)
Async XLA Ops:
  6.5 24.9 %copy-start.1 = (s32[2,20,4,3]{1,2,3,0:T(4,128)S(1)}, s32[2,20,4,3]{1,2,3,0:T(4,128)}, u32[]{:S(2)}) copy-start(s32[2,20,4,3]{1,2,3,0:T(4,128)} %param.7) | copy-start | bytes 5764
  6.5 464.7 %reduce-scatter.4.cloned.1.call-start = ((), (), s32[]{:S(2)}) async-start(), calls=%async_computation.1 | async-start | bytes 14413824
  148.0 70.7 %copy-start = (bf16[48,2,4,529]{3,2,1,0:T(4,128)(2,1)S(1)}, bf16[48,2,4,529]{3,2,1,0:T(4,128)(2,1)}, u32[]{:S(2)}) copy-start(bf16[48,2,4,529]{3,2,1,0:T(4,128)(2,1)} %param.4) | copy-start | bytes 1218820
  148.0 75.9 %copy-start.2 = (s32[48,2,4]{0,2,1:T(4,128)S(1)}, s32[48,2,4]{0,2,1:T(4,128)}, u32[]{:S(2)}) copy-start(s32[48,2,4]{0,2,1:T(4,128)} %param.5) | copy-start | bytes 4612
Sparse Core Ops, SparseCore 0:
  329.0 142.1 reduce-scatter.3
